TPU v7x, 16 devices: a 4x2x1 block of a 4x4x8 slice. The times are simulated.
16 devices in a mesh: dp: 2 (over y, z), sh: 8 (over x, core).
Axes of the slice: x: 4, y: 2, z: 1, core: 2. Of those that a mesh axis runs over, the one named last changes fastest.
The devices are a block of a 4x4x8 slice.
Arguments:
- k_prefill: bfloat16 [16, 4352, 8, 128], P('dp', None, 'sh'), parts along dimension 0
- v_prefill: bfloat16 [16, 4352, 8, 128], P('dp', None, 'sh'), parts along dimension 0
- lengths: int32 [16], P('dp'), parts along dimension 0
- residual: bfloat16 [16, 4096], P(('dp', 'sh')), parts along dimension 0
- norm_gain: bfloat16 [4096], replicated
- w_query: bfloat16 [4096, 4096], replicated
- w_key: bfloat16 [4096, 1024], replicated
- w_value: bfloat16 [4096, 1024], replicated
- w_out: bfloat16 [4096, 4096], replicated
Outputs:
- output 1: bfloat16 [16, 4096], P(('dp', 'sh')), parts along dimension 0
- output 2: bfloat16 [16, 4096, 8, 128], P(('dp', 'sh')), parts along dimension 0
- output 3: bfloat16 [16, 4096, 8, 128], P(('dp', 'sh')), parts along dimension 0
There are 2 independent parts. A program takes and returns all parts, laid end to end along the dimension named above; an argument that names none is the same for every part.
All inputs are finite; a program needn't handle non-finite values.
Results may differ from a plain program's by a relative error of at most 0.00417.
Values are sent between devices in bfloat16 or wider.
A program may use at most 768 MiB of HBM per device.

v0:
```python
import jax
import jax.numpy as jnp
from jax import lax
from jax.sharding import PartitionSpec as P

WINDOW = 4096
THETA = 10000.0
EPS = 1e-5


def rolling_rows(prefill, lengths):
    def one_row(row_vals, row_len):
        first_pos = jnp.maximum(row_len - WINDOW, 0)
        win_vals = lax.dynamic_slice_in_dim(row_vals, first_pos, WINDOW, axis=0)
        positions = first_pos + jnp.arange(WINDOW, dtype=jnp.int32)
        win_vals = jnp.where((positions < row_len)[:, None, None], win_vals, jnp.zeros((), win_vals.dtype))
        doubled = jnp.concatenate([win_vals, win_vals], axis=0)
        return lax.dynamic_slice_in_dim(doubled, WINDOW - first_pos % WINDOW, WINDOW, axis=0)
    return jax.vmap(one_row)(prefill, lengths)


def rotate(heads, positions):
    head_dim = heads.shape[-1]
    half_dim = head_dim // 2
    inv_freq = THETA ** (-2.0 * jnp.arange(half_dim, dtype=jnp.float32) / head_dim)
    angles = positions.astype(jnp.float32).reshape(positions.shape + (1,) * (heads.ndim - 1)) * inv_freq
    cos_part = jnp.cos(angles)
    sin_part = jnp.sin(angles)
    first_half = heads[..., :half_dim].astype(jnp.float32)
    second_half = heads[..., half_dim:].astype(jnp.float32)
    return jnp.concatenate([first_half * cos_part - second_half * sin_part, second_half * cos_part + first_half * sin_part], axis=-1).astype(jnp.bfloat16)


def decode_rows(residual, lengths, k_cache, v_cache, norm_gain, w_query, w_key, w_value, w_out):
    num_rows = residual.shape[0]
    kv_heads = k_cache.shape[2]
    head_dim = k_cache.shape[3]
    q_group = w_query.shape[1] // (kv_heads * head_dim)
    resid_f32 = residual.astype(jnp.float32)
    inv_rms = lax.rsqrt(jnp.mean(resid_f32 * resid_f32, axis=-1, keepdims=True) + EPS)
    normed = (resid_f32 * inv_rms * norm_gain.astype(jnp.float32)).astype(jnp.bfloat16)
    q_heads = jnp.dot(normed, w_query, preferred_element_type=jnp.float32).astype(jnp.bfloat16).reshape(num_rows, kv_heads, q_group, head_dim)
    k_new = jnp.dot(normed, w_key, preferred_element_type=jnp.float32).astype(jnp.bfloat16).reshape(num_rows, kv_heads, head_dim)
    v_new = jnp.dot(normed, w_value, preferred_element_type=jnp.float32).astype(jnp.bfloat16).reshape(num_rows, kv_heads, head_dim)
    q_heads = rotate(q_heads, lengths)
    k_new = rotate(k_new, lengths)
    slot_ids = jnp.arange(WINDOW, dtype=jnp.int32)
    new_slot = (slot_ids[None, :] == (lengths % WINDOW)[:, None])[:, :, None, None]
    k_cache = jnp.where(new_slot, k_new[:, None], k_cache)
    v_cache = jnp.where(new_slot, v_new[:, None], v_cache)
    live_slot = (lengths[:, None] - jnp.remainder(lengths[:, None] - slot_ids[None, :], WINDOW)) >= 0
    scores = jnp.einsum('rkgd,rwkd->rkgw', q_heads, k_cache, preferred_element_type=jnp.float32) / head_dim ** 0.5
    scores = jnp.where(live_slot[:, None, None, :], scores, -jnp.inf)
    exp_scores = jnp.exp(scores - jnp.max(scores, axis=-1, keepdims=True))
    weights = (exp_scores / jnp.sum(exp_scores, axis=-1, keepdims=True)).astype(jnp.bfloat16)
    attn_out = jnp.einsum('rkgw,rwkd->rkgd', weights, v_cache, preferred_element_type=jnp.float32).astype(jnp.bfloat16).reshape(num_rows, kv_heads * q_group * head_dim)
    resid_out = (resid_f32 + jnp.dot(attn_out, w_out, preferred_element_type=jnp.float32)).astype(jnp.bfloat16)
    return resid_out, k_cache, v_cache


def solution(mesh):
    head_spec = P('dp', None, 'sh', None)
    row_spec = P(('dp', 'sh'))
    full_spec = P(None, None)

    def per_device(k_prefill, v_prefill, lengths, residual, norm_gain, w_query, w_key, w_value, w_out):
        num_rows = residual.shape[0]
        my_lengths = lax.dynamic_slice_in_dim(lengths, lax.axis_index('sh') * num_rows, num_rows)
        k_rows = lax.all_to_all(k_prefill, 'sh', 0, 2, tiled=True)
        v_rows = lax.all_to_all(v_prefill, 'sh', 0, 2, tiled=True)
        k_cache = rolling_rows(k_rows, my_lengths)
        v_cache = rolling_rows(v_rows, my_lengths)
        return decode_rows(residual, my_lengths, k_cache, v_cache, norm_gain, w_query, w_key, w_value, w_out)
    return jax.shard_map(per_device, mesh=mesh, in_specs=(head_spec, head_spec, P('dp'), P(('dp', 'sh'), None), P(None), full_spec, full_spec, full_spec, full_spec), out_specs=(P(('dp', 'sh'), None), row_spec, row_spec), check_vma=False)
```

profile of v0, /device:TPU:112, one launch (start us, length us, event | category | flops | bytes accessed | tf_op | source)
XLA Modules:
  0.0 376.9 jit_solution(15413200151383528971)
XLA Ops:
  0.6 106.2 %all_to_all.36 = bf16[8,4352,1,128]{3,1,2,0:T(8,128)(2,1)} all-to-all(bf16[8,4352,1,128]{3,1,2,0:T(8,128)(2,1)} %param.9), channel_id=1, replica_groups=mesh['dp'=2,'sh'=8] {'sh'}, dimensions={0} | all-to-all | bytes 17825792 | tf_op jit(solution)/shard_map/all_to_all | solution.py:69
  106.8 0.0 copy-start.2
  106.8 0.0 copy-start.1
  106.8 0.0 copy-start
  106.8 5.3 %all-to-all-start.1 = ((bf16[8,4352,1,128]{3,1,2,0:T(8,128)(2,1)}), bf16[8,4352,1,128]{3,1,2,0:T(8,128)(2,1)}, u32[]{:S(2)}, u32[]{:S(2)}) async-start(bf16[8,4352,1,128]{3,1,2,0:T(8,128)(2,1)} %param.10), calls=%async_computation.1 | async-start | bytes 17825792 | tf_op jit(solution)/shard_map/all_to_all | solution.py:70
  112.2 0.0 copy-done.2
  112.2 0.6 dynamic_slice.3
  116.0 0.0 copy-done.1
  116.0 0.0 copy-done
  116.0 0.6 multiply_reduce_fusion
  117.4 12.8 %fusion.31 = f32[1,4096]{1,0:T(1,128)S(1)} fusion(bf16[4096,4096]{1,0:T(8,128)(2,1)} %param.14, f32[1,4096]{1,0:T(1,128)S(1)} %bitcast.54, bf16[1,4096]{1,0:T(2,128)(2,1)S(1)} %copy-done, f32[]{:T(128)S(6)} %rsqrt.4), kind=kOutput, calls=%fused_computation.44 | convolution fusion | flops 33570816 | bytes 33595396 | tf_op jit(solution)/shard_map/dot_general | solution.py:42
  130.2 0.0 slice-start
  130.2 0.1 fusion.50
  130.3 0.0 slice-start.1
  130.3 4.7 %fusion.29 = f32[1,1024]{1,0:T(1,128)S(1)} fusion(bf16[4096,1024]{1,0:T(8,128)(2,1)} %param.15, f32[1,4096]{1,0:T(1,128)S(1)} %bitcast.55, bf16[1,4096]{1,0:T(2,128)(2,1)S(1)} %copy-done, f32[]{:T(128)S(6)} %rsqrt.4), kind=kOutput, calls=%fused_computation.42 | convolution fusion | flops 8404992 | bytes 8417284 | tf_op jit(solution)/shard_map/dot_general | solution.py:43
  135.0 0.1 fusion.49
  135.1 0.1 pad_maximum_fusion
  135.2 0.7 fusion.26
  135.9 0.7 add_compare_fusion
  136.5 0.0 slice-done
  136.6 0.0 slice-done.1
  136.6 1.2 fusion.27
  137.8 0.1 fusion.40
  137.9 9.0 %constant_dynamic-slice_fusion.1 = bf16[8,4096,1,128]{3,1,2,0:T(8,128)(2,1)} fusion(bf16[8,4352,1,128]{3,1,2,0:T(8,128)(2,1)} %all_to_all.36, s32[]{:T(128)} %bitcast.12), kind=kLoop, calls=%fused_computation.75 | loop fusion | bytes 16777220
  146.8 65.3 %all-to-all-done.1 = bf16[8,4352,1,128]{3,1,2,0:T(8,128)(2,1)} async-done(((bf16[8,4352,1,128]{3,1,2,0:T(8,128)(2,1)}), bf16[8,4352,1,128]{3,1,2,0:T(8,128)(2,1)}, u32[]{:S(2)}, u32[]{:S(2)}) %all-to-all-start.1) | async-done | bytes 8912928 | tf_op jit(solution)/shard_map/all_to_all | solution.py:70
  212.1 8.9 %constant_dynamic-slice_fusion = bf16[8,4096,1,128]{3,1,2,0:T(8,128)(2,1)} fusion(bf16[8,4352,1,128]{3,1,2,0:T(8,128)(2,1)} %all-to-all-done.1, s32[]{:T(128)} %bitcast.12), kind=kLoop, calls=%fused_computation.74 | loop fusion | bytes 16777220
  221.1 35.0 %bitcast_select_fusion.1 = (bf16[1,4096,8,128]{3,2,1,0:T(8,128)(2,1)S(1)}, bf16[1,4096,8,128]{3,2,1,0:T(8,128)(2,1)S(1)}) fusion(bf16[8,4096,1,128]{3,1,2,0:T(8,128)(2,1)} %constant_dynamic-slice_fusion.1, pred[4096]{0:T(1024)(128)(4,1)S(1)} %add_compare_fusion, bf16[8,4096,1,128]{3,1,2,0:T(8,128)(2,1)} %constant_dynamic-slice_fusion), kind=kLoop, calls=%fused_computation.8 | loop fusion | flops 8388608 | bytes 33558528 | tf_op jit(solution)/shard_map/vmap(jit(_where))/select_n | solution.py:16
  256.1 48.0 %bitcast_select_fusion.3 = (bf16[4096,8,128]{2,1,0:T(8,128)(2,1)}, bf16[4096,8,128]{2,1,0:T(8,128)(2,1)}) fusion(pred[4096]{0:T(1024)(128)(4,1)S(1)} %iota_compare_fusion, bf16[8,128]{1,0:T(8,128)(2,1)S(1)} %pad_maximum_fusion, s32[]{:T(128)} %bitcast.16, bf16[1,4096,8,128]{3,2,1,0:T(8,128)(2,1)S(1)} %get-tuple-element.53, ...), kind=kLoop, calls=%fused_computation.10 | loop fusion | flops 16777216 | bytes 33562628 | tf_op jit(solution)/shard_map/jit(_where)/select_n | solution.py:49
  304.1 47.8 %broadcast_select_fusion = (bf16[1,4096,8,128]{3,2,1,0:T(8,128)(2,1)}, bf16[1,4096,8,128]{3,2,1,0:T(8,128)(2,1)}) fusion(pred[4096]{0:T(1024)(128)(4,1)S(1)} %iota_compare_fusion, bf16[8,128]{1,0:T(8,128)(2,1)S(1)} %convert_bitcast_fusion, s32[]{:T(128)} %bitcast.16, bf16[1,4096,8,128]{3,2,1,0:T(8,128)(2,1)S(1)} %get-tuple-element.54, ...), kind=kLoop, calls=%fused_computation.15 | loop fusion | flops 16777216 | bytes 33562628 | tf_op jit(solution)/shard_map/jit(_where)/select_n | solution.py:50
  351.9 5.9 %fusion.53 = (f32[8,4]{1,0:T(8,128)S(1)}, f32[8,4,4096]{2,1,0:T(4,128)S(1)}) fusion(bf16[4096,8,128]{2,1,0:T(8,128)(2,1)} %get-tuple-element.51, pred[4096]{0:T(1024)(128)(4,1)S(1)} %fusion.26, bf16[8,4,64]{2,1,0:T(4,128)(2,1)S(1)} %get-tuple-element.48, bf16[8,4,64]{2,1,0:T(4,128)(2,1)S(1)} %get-tuple-element.47), kind=kOutput, calls=%fused_computation.80 | convolution fusion | flops 34099200 | bytes 8925312 | tf_op jit(solution)/shard_map/sub | solution.py:54
  357.8 5.7 %fusion.16 = bf16[8,4,128]{2,1,0:T(4,128)(2,1)S(1)} fusion(bf16[4096,8,128]{2,1,0:T(8,128)(2,1)} %get-tuple-element.52, f32[8,4,4096]{2,1,0:T(4,128)S(1)} %get-tuple-element.58, f32[8,4]{1,0:T(8,128)S(1)} %get-tuple-element.57), kind=kOutput, calls=%fused_computation.23 | convolution fusion | flops 33820672 | bytes 8921216 | tf_op jit(solution)/shard_map/rkgw,rwkd->rkgd/dot_general | solution.py:56
  363.5 13.4 %fusion.15 = bf16[1,4096]{1,0:T(2,128)(2,1)} fusion(bf16[4096,1]{0,1:T(2,128)(2,1)S(1)} %reshape.377, bf16[4096,4096]{1,0:T(8,128)(2,1)} %param.17, bf16[1,4096]{1,0:T(2,128)(2,1)S(1)} %copy-done), kind=kOutput, calls=%fused_computation.22 | convolution fusion | flops 33566720 | bytes 33579008 | tf_op jit(solution)/shard_map/dot_general | solution.py:57
  (7 shorter events, 0.0 us)
Async XLA Ops:
  106.8 5.3 %copy-start.2 = (s32[8]{0:T(128)S(1)}, s32[8]{0:T(128)}, u32[]{:S(2)}) copy-start(s32[8]{0:T(128)} %param.11) | copy-start | bytes 100
  106.8 9.2 %copy-start.1 = (bf16[4096]{0:T(1024)(128)(2,1)S(1)}, bf16[4096]{0:T(1024)(128)(2,1)}, u32[]{:S(2)}) copy-start(bf16[4096]{0:T(1024)(128)(2,1)} %param.13) | copy-start | bytes 24580
  106.8 9.2 %copy-start = (bf16[1,4096]{1,0:T(2,128)(2,1)S(1)}, bf16[1,4096]{1,0:T(2,128)(2,1)}, u32[]{:S(2)}) copy-start(bf16[1,4096]{1,0:T(2,128)(2,1)} %param.12) | copy-start | bytes 24580
  106.8 105.3 %all-to-all-start.1 = ((bf16[8,4352,1,128]{3,1,2,0:T(8,128)(2,1)}), bf16[8,4352,1,128]{3,1,2,0:T(8,128)(2,1)}, u32[]{:S(2)}, u32[]{:S(2)}) async-start(bf16[8,4352,1,128]{3,1,2,0:T(8,128)(2,1)} %param.10), calls=%async_computation.1 | async-start | bytes 17825792 | tf_op jit(solution)/shard_map/all_to_all | solution.py:70
  130.2 6.3 %slice-start = ((s8[8388608]{0:T(1024)(128)(4,1)}), s8[4194304]{0:T(1024)(128)(4,1)S(1)}, s32[]{:S(2)}) async-start(s8[8388608]{0:T(1024)(128)(4,1)} %bitcast.52), calls=%async_computation.2 | async-start | bytes 8388608
  130.3 6.3 %slice-start.1 = ((s8[8388608]{0:T(1024)(128)(4,1)}), s8[4194304]{0:T(1024)(128)(4,1)S(1)}, s32[]{:S(2)}) async-start(s8[8388608]{0:T(1024)(128)(4,1)} %bitcast.52), calls=%async_computation.3 | async-start | bytes 8388608
where the time goes:
time: 377 us
  other arithmetic  133 us (35%)
  blocking collectives  106 us (28%)
  waiting for transfers between devices  65.3 us (17%)
  matrix products  43.8 us (12%)
  local copies, waits for them, and re-layouts  18.5 us (5%)
  starting transfers between devices  5.33 us (1%)
  between operations  4.73 us (1%)
    all_to_all x1, blocking collectives, per_device(): k_rows = lax.all_to_all(k_prefill, 'sh', 0, 2, tiled=True)  106 us
    all_to_all x1, waiting for transfers between devices, per_device(): v_rows = lax.all_to_all(v_prefill, 'sh', 0, 2, tiled=True)  65.3 us
    select_n x1, other arithmetic, decode_rows(): k_cache = jnp.where(new_slot, k_new[:, None], k_cache)  48 us
    select_n x1, other arithmetic, decode_rows(): v_cache = jnp.where(new_slot, v_new[:, None], v_cache)  47.8 us
    select_n x1, other arithmetic, one_row(): jnp.where((positions < row_len)[:, None, None], win_vals, jnp.zeros((), w...  35 us
    unnamed x12, local copies, waits for them, and re-layouts  17.9 us
    dot_general x1, matrix products, decode_rows(): jnp.dot(attn_out, w_out, preferred_element_type=jnp.float32)  13.4 us
    dot_general x1, matrix products, decode_rows(): jnp.dot(normed, w_query, preferred_element_type=jnp.float32)  12.8 us
  transfers between devices with their start and end apart: 1, of which 1 were waited for; matrix products, arithmetic and copies ran while one was open for 8% of the time, Pallas kernels for 0%

commit v1 on v0

--- a/solution.py
+++ b/solution.py
@@ -1,22 +1,16 @@
+import functools
+
 import jax
 import jax.numpy as jnp
 from jax import lax
+from jax.experimental import pallas as pl
+from jax.experimental.pallas import tpu as pltpu
 from jax.sharding import PartitionSpec as P
 
 WINDOW = 4096
 THETA = 10000.0
 EPS = 1e-5
-
-
-def rolling_rows(prefill, lengths):
-    def one_row(row_vals, row_len):
-        first_pos = jnp.maximum(row_len - WINDOW, 0)
-        win_vals = lax.dynamic_slice_in_dim(row_vals, first_pos, WINDOW, axis=0)
-        positions = first_pos + jnp.arange(WINDOW, dtype=jnp.int32)
-        win_vals = jnp.where((positions < row_len)[:, None, None], win_vals, jnp.zeros((), win_vals.dtype))
-        doubled = jnp.concatenate([win_vals, win_vals], axis=0)
-        return lax.dynamic_slice_in_dim(doubled, WINDOW - first_pos % WINDOW, WINDOW, axis=0)
-    return jax.vmap(one_row)(prefill, lengths)
+MESH = pl.DeviceIdType.MESH
 
 
 def rotate(heads, positions):
@@ -46,9 +40,10 @@
     k_new = rotate(k_new, lengths)
     slot_ids = jnp.arange(WINDOW, dtype=jnp.int32)
     new_slot = (slot_ids[None, :] == (lengths % WINDOW)[:, None])[:, :, None, None]
-    k_cache = jnp.where(new_slot, k_new[:, None], k_cache)
-    v_cache = jnp.where(new_slot, v_new[:, None], v_cache)
-    live_slot = (lengths[:, None] - jnp.remainder(lengths[:, None] - slot_ids[None, :], WINDOW)) >= 0
+    held = (slot_ids[None, :] < lengths[:, None])[:, :, None, None]
+    k_cache = jnp.where(new_slot, k_new[:, None], jnp.where(held, k_cache, 0))
+    v_cache = jnp.where(new_slot, v_new[:, None], jnp.where(held, v_cache, 0))
+    live_slot = slot_ids[None, :] <= lengths[:, None]
     scores = jnp.einsum('rkgd,rwkd->rkgw', q_heads, k_cache, preferred_element_type=jnp.float32) / head_dim ** 0.5
     scores = jnp.where(live_slot[:, None, None, :], scores, -jnp.inf)
     exp_scores = jnp.exp(scores - jnp.max(scores, axis=-1, keepdims=True))
@@ -58,17 +53,63 @@
     return resid_out, k_cache, v_cache
 
 
+def exchange_kernel(n, rows, over, k_over, v_over, k_in, v_in, k_out, v_out, send_sem, recv_sem, own_sem):
+    me = lax.axis_index('sh')
+    window = k_out.shape[1]
+    barrier = pltpu.get_barrier_semaphore()
+    for d in range(1, n):
+        pl.semaphore_signal(barrier, inc=1, device_id={'sh': lax.rem(me + d, n)}, device_id_type=MESH)
+    pl.semaphore_wait(barrier, n - 1)
+    parts = ((k_over, k_out, 0, over), (v_over, v_out, 0, over), (k_in, k_out, over, window - over), (v_in, v_out, over, window - over))
+    copies = []
+    for p, (src, dst, first, size) in enumerate(parts):
+        for d in (2, 6, 3, 5, 4, 7, 1):
+            peer = lax.rem(me + d, n)
+            copy = pltpu.make_async_remote_copy(
+                src_ref=src.at[peer, pl.ds(first, size)], dst_ref=dst.at[me, pl.ds(first, size)],
+                send_sem=send_sem.at[d, p], recv_sem=recv_sem.at[d, p], device_id={'sh': peer}, device_id_type=MESH)
+            copy.start()
+            copies.append(copy)
+        own = pltpu.make_async_copy(src.at[me, pl.ds(first, size)], dst.at[me, pl.ds(first, size)], own_sem.at[p])
+        own.start()
+        copies.append(own)
+    for copy in copies:
+        copy.wait()
+
+
+def exchange(n, k_rows, v_rows, k_over, v_over):
+    rows, _, head_dim = k_rows.shape
+    out = jax.ShapeDtypeStruct((n, WINDOW, head_dim), k_rows.dtype)
+    any_spec = pl.BlockSpec(memory_space=pl.ANY)
+    return pl.pallas_call(
+        functools.partial(exchange_kernel, n, rows, k_over.shape[1]),
+        out_shape=(out, out),
+        in_specs=[any_spec] * 4,
+        out_specs=(any_spec, any_spec),
+        scratch_shapes=[pltpu.SemaphoreType.DMA((n, 4)), pltpu.SemaphoreType.DMA((n, 4)), pltpu.SemaphoreType.DMA((4,))],
+        compiler_params=pltpu.CompilerParams(collective_id=0, has_side_effects=True),
+        name='exchange',
+    )(k_over, v_over, k_rows, v_rows)
+
+
 def solution(mesh):
     head_spec = P('dp', None, 'sh', None)
     row_spec = P(('dp', 'sh'))
     full_spec = P(None, None)
+    n = mesh.shape['sh']
 
     def per_device(k_prefill, v_prefill, lengths, residual, norm_gain, w_query, w_key, w_value, w_out):
         num_rows = residual.shape[0]
+        rows, seq, _, head_dim = k_prefill.shape
         my_lengths = lax.dynamic_slice_in_dim(lengths, lax.axis_index('sh') * num_rows, num_rows)
-        k_rows = lax.all_to_all(k_prefill, 'sh', 0, 2, tiled=True)
-        v_rows = lax.all_to_all(v_prefill, 'sh', 0, 2, tiled=True)
-        k_cache = rolling_rows(k_rows, my_lengths)
-        v_cache = rolling_rows(v_rows, my_lengths)
+        k_rows = k_prefill.reshape(rows, seq, head_dim)
+        v_rows = v_prefill.reshape(rows, seq, head_dim)
+        over = seq - WINDOW
+        wraps = (jnp.arange(over, dtype=jnp.int32)[None, :] < lengths[:, None] - WINDOW)[:, :, None]
+        k_over = jnp.where(wraps, k_rows[:, WINDOW:], k_rows[:, :over])
+        v_over = jnp.where(wraps, v_rows[:, WINDOW:], v_rows[:, :over])
+        k_heads, v_heads = exchange(n, k_rows, v_rows, k_over, v_over)
+        k_cache = k_heads.transpose(1, 0, 2)[None]
+        v_cache = v_heads.transpose(1, 0, 2)[None]
         return decode_rows(residual, my_lengths, k_cache, v_cache, norm_gain, w_query, w_key, w_value, w_out)
     return jax.shard_map(per_device, mesh=mesh, in_specs=(head_spec, head_spec, P('dp'), P(('dp', 'sh'), None), P(None), full_spec, full_spec, full_spec, full_spec), out_specs=(P(('dp', 'sh'), None), row_spec, row_spec), check_vma=False)

time: 377 us -> 302 us (0.80)
  Pallas kernels: 0 us -> 187 us
  other arithmetic: 133 us -> 13.5 us
  blocking collectives: 106 us -> 0 us
  waiting for transfers between devices: 65.3 us -> 0 us
  local copies, waits for them, and re-layouts: 18.5 us -> 51.9 us
  starting transfers between devices: 5.33 us -> 0 us
    pallas_call x0 -> x1, Pallas kernels: none -> 187 us  [exchange(): pl.pallas_call(functools.partial(exchange_kernel, n, rows, k_over.shape[1...]
    select_n x3 -> x2, other arithmetic: 131 us -> 9.7 us  [the longest x1 7.17 us: decode_rows(): v_cache = jnp.where(new_slot, v_new[:, None], jnp.where(held, v_cache, 0))]
    all_to_all x1 -> x0, blocking collectives: 106 us -> none  [per_device(): k_rows = lax.all_to_all(k_prefill, 'sh', 0, 2, tiled=True)]
    all_to_all x1 -> x0, waiting for transfers between devices: 65.3 us -> none  [per_device(): v_rows = lax.all_to_all(v_prefill, 'sh', 0, 2, tiled=True)]
    unnamed x12 -> x10, local copies, waits for them, and re-layouts: 17.9 us -> 50.5 us
    all_to_all x1 -> x0, starting transfers between devices: 5.33 us -> none  [per_device(): v_rows = lax.all_to_all(v_prefill, 'sh', 0, 2, tiled=True)]
  transfers between devices with their start and end apart: 1 -> 0, of which waited for: 1 -> 0; matrix products, arithmetic and copies ran while one was open for 8% -> 0% of each run, Pallas kernels for 0% -> 0%
where the time goes in v1:
time: 302 us; the launch traced here: 301 us
  Pallas kernels  187 us (62%)
  local copies, waits for them, and re-layouts  51.9 us (17%)
  matrix products  44.8 us (15%)
  other arithmetic  13.5 us (4%)
  between operations  4.02 us (1%)
    pallas_call x1, Pallas kernels, exchange(): pl.pallas_call(functools.partial(exchange_kernel, n, rows, k_over.shape[1...  187 us
    unnamed x10, local copies, waits for them, and re-layouts  50.5 us
    dot_general x1, matrix products, decode_rows(): jnp.dot(attn_out, w_out, preferred_element_type=jnp.float32)  13.4 us
    dot_general x1, matrix products, decode_rows(): jnp.dot(normed, w_query, preferred_element_type=jnp.float32)  12.8 us
    select_n x1, other arithmetic, decode_rows(): v_cache = jnp.where(new_slot, v_new[:, None], jnp.where(held, v_cache, 0))  7.17 us
    sub x1, matrix products, decode_rows(): exp_scores = jnp.exp(scores - jnp.max(scores, axis=-1, keepdims=True))  6.78 us

profile of v1, /device:TPU:112, one launch (start us, length us, event | category | flops | bytes accessed | tf_op | source)
XLA Modules:
  0.0 301.1 jit_solution(9580043453324675043)
XLA Ops:
  0.6 0.0 copy-start.1
  0.6 1.4 multiply_reduce_fusion
  2.8 0.0 slice-start
  2.8 1.4 dynamic_slice.3
  6.8 0.7 broadcast_add_fusion
  7.5 0.1 iota_compare_fusion.3
  7.6 0.7 iota_compare_fusion
  8.2 0.7 broadcast_in_dim.102
  8.9 0.0 slice-start.1
  8.9 4.7 %fusion.24 = f32[1,1024]{1,0:T(1,128)S(1)} fusion(bf16[4096,1024]{1,0:T(8,128)(2,1)} %param.15, f32[1,4096]{1,0:T(1,128)S(1)} %bitcast.62, bf16[1,4096]{1,0:T(2,128)(2,1)} %param.12, f32[]{:T(128)S(6)} %rsqrt.4), kind=kOutput, calls=%fused_computation.28 | convolution fusion | flops 8404992 | bytes 8417284 | tf_op jit(solution)/shard_map/dot_general | solution.py:37
  13.7 0.1 fusion.41
  13.7 0.1 pad_maximum_fusion
  13.8 0.0 copy-done.1
  13.8 0.0 slice-done
  13.8 0.0 slice-done.1
  13.9 1.2 fusion.22
  15.0 12.8 %fusion.26 = f32[1,4096]{1,0:T(1,128)S(1)} fusion(bf16[4096,4096]{1,0:T(8,128)(2,1)} %param.14, f32[1,4096]{1,0:T(1,128)S(1)} %bitcast.64, bf16[1,4096]{1,0:T(2,128)(2,1)S(1)} %copy-done.1, f32[]{:T(128)S(6)} %rsqrt.4), kind=kOutput, calls=%fused_computation.30 | convolution fusion | flops 33570816 | bytes 33595396 | tf_op jit(solution)/shard_map/dot_general | solution.py:36
  27.9 0.1 fusion.32
  28.0 2.5 slice_select_fusion
  30.5 186.9 %exchange.1 = (bf16[8,4096,128]{2,1,0:T(8,128)(2,1)}, bf16[8,4096,128]{2,1,0:T(8,128)(2,1)}) custom-call(bf16[8,256,128]{2,1,0:T(8,128)(2,1)} %get-tuple-element.17.k_over, bf16[8,256,128]{2,1,0:T(8,128)(2,1)} %get-tuple-element.16.v_over, bf16[8,4352,128]{2,1,0:T(8,128)(2,1)} %bitcast.61, bf16[8,4352,128]{2,1,0:T(8,128)(2,1)} %bitcast.59), custom_call_target="tpu_custom_call" | custom-call | tf_op jit(solution)/shard_map/exchange/pallas_call | solution.py:84
  217.4 6.8 %fusion.47 = (f32[8,4]{1,0:T(8,128)S(1)}, f32[8,4,4096]{2,1,0:T(4,128)S(1)}) fusion(pred[4096]{0:T(1024)(128)(4,1)S(1)} %get-tuple-element.21, bf16[8,4,64]{2,1,0:T(4,128)(2,1)S(1)} %get-tuple-element.11, bf16[8,4,64]{2,1,0:T(4,128)(2,1)S(1)} %get-tuple-element.10, bf16[8,4096,128]{2,1,0:T(8,128)(2,1)} %get-tuple-element.5, ...), kind=kOutput, calls=%fused_computation.66 | convolution fusion | flops 42487808 | bytes 8935552 | tf_op jit(solution)/shard_map/sub | solution.py:49
  224.2 0.0 copy-start
  224.2 5.8 %fusion.14 = bf16[8,4,128]{2,1,0:T(4,128)(2,1)S(1)} fusion(f32[8,4,4096]{2,1,0:T(4,128)S(1)} %get-tuple-element.19, f32[8,4]{1,0:T(8,128)S(1)} %get-tuple-element.18, bf16[8,4096,128]{2,1,0:T(8,128)(2,1)} %get-tuple-element.6, pred[4096]{0:T(1024)(128)(4,1)S(1)} %get-tuple-element.20, pred[4096]{0:T(1024)(128)(4,1)S(1)} %iota_compare_fusion.1, ...), kind=kOutput, calls=%fused_computation.13 | convolution fusion | flops 42209280 | bytes 8931456 | tf_op jit(solution)/shard_map/rkgw,rwkd->rkgd/dot_general | solution.py:51
  230.0 0.1 copy-done
  230.1 7.2 %fusion.46 = (bf16[1,4096,8,128]{3,1,2,0:T(8,128)(2,1)S(1)}, bf16[1,4096,8,128]{3,1,2,0:T(8,128)(2,1)S(1)}) fusion(bf16[8,4096,128]{2,1,0:T(8,128)(2,1)} %get-tuple-element.6, pred[4096]{0:T(1024)(128)(4,1)S(1)} %get-tuple-element.20, bf16[8,128]{1,0:T(8,128)(2,1)S(1)} %convert_bitcast_fusion, pred[4096]{0:T(1024)(128)(4,1)S(1)} %iota_compare_fusion.1, ...), kind=kLoop, calls=%fused_computation.65 | loop fusion | flops 16777216 | bytes 33566720 | tf_op jit(solution)/shard_map/jit(_where)/select_n | solution.py:45
  237.3 25.3 %copy.13 = bf16[1,4096,8,128]{3,2,1,0:T(8,128)(2,1)} copy(bf16[1,4096,8,128]{3,1,2,0:T(8,128)(2,1)S(1)} %get-tuple-element.12) | data formatting | bytes 16777216
  262.6 13.4 %fusion.13 = bf16[1,4096]{1,0:T(2,128)(2,1)} fusion(bf16[4096,1]{0,1:T(2,128)(2,1)S(1)} %reshape.232, bf16[4096,4096]{1,0:T(8,128)(2,1)} %param.17, bf16[1,4096]{1,0:T(2,128)(2,1)S(1)} %copy-done.1), kind=kOutput, calls=%fused_computation.12 | convolution fusion | flops 33566720 | bytes 33579008 | tf_op jit(solution)/shard_map/dot_general | solution.py:52
  276.0 25.1 %copy.12 = bf16[1,4096,8,128]{3,2,1,0:T(8,128)(2,1)} copy(bf16[1,4096,8,128]{3,1,2,0:T(8,128)(2,1)S(1)} %get-tuple-element.13) | data formatting | bytes 16777216
  (7 shorter events, 0.1 us)
Async XLA Ops:
  0.6 13.2 %copy-start.1 = (bf16[1,4096]{1,0:T(2,128)(2,1)S(1)}, bf16[1,4096]{1,0:T(2,128)(2,1)}, u32[]{:S(2)}) copy-start(bf16[1,4096]{1,0:T(2,128)(2,1)} %param.12) | copy-start | bytes 24580
  2.8 11.1 %slice-start = ((s8[8388608]{0:T(1024)(128)(4,1)}), s8[4194304]{0:T(1024)(128)(4,1)S(1)}, s32[]{:S(2)}) async-start(s8[8388608]{0:T(1024)(128)(4,1)} %bitcast.56), calls=%async_computation | async-start | bytes 8388608
  8.9 4.9 %slice-start.1 = ((s8[8388608]{0:T(1024)(128)(4,1)}), s8[4194304]{0:T(1024)(128)(4,1)S(1)}, s32[]{:S(2)}) async-start(s8[8388608]{0:T(1024)(128)(4,1)} %bitcast.56), calls=%async_computation.1 | async-start | bytes 8388608
  224.2 5.9 %copy-start = (bf16[8,4096,128]{2,1,0:T(8,128)(2,1)S(1)}, bf16[8,4096,128]{2,1,0:T(8,128)(2,1)}, u32[]{:S(2)}) copy-start(bf16[8,4096,128]{2,1,0:T(8,128)(2,1)} %get-tuple-element.5) | copy-start | bytes 25165828

commit v2 on v0

v2 whole, which is shorter than its diff:
```python
import functools

import jax
import jax.numpy as jnp
from jax import lax
from jax.experimental import pallas as pl
from jax.experimental.pallas import tpu as pltpu
from jax.sharding import PartitionSpec as P

WINDOW = 4096
THETA = 10000.0
EPS = 1e-5
MESH = pl.DeviceIdType.MESH


def levels(group):
    nblk = WINDOW // group
    return tuple(range(nblk // 2 + 1, nblk + 1))


def exchange_kernel(n, group, half, len_ref, x_ref, g_ref, cos_ref, sin_ref, k_in, v_in, wq, wk, wv,
                    k_out, v_out, flat, k_new, v_new,
                    over_a, over_b, staged, kv_buf, wbuf, normed, proj, proj2, q_heads, scores, probs, p_new, acc, k_rows32,
                    send_sem, recv_sem, own_sem, fsend_sem, frecv_sem, over_sem, stage_sem, w_sem, kv_sem):
    me = lax.axis_index('sh')
    mate = me + 1 - 2 * lax.rem(me, 2)
    heads, q_group, head_dim = q_heads.shape
    over = over_a.shape[2]
    nblk = WINDOW // group
    first = 2 * half - nblk
    nst = half - first
    barrier = pltpu.get_barrier_semaphore()
    for d in range(1, n):
        pl.semaphore_signal(barrier, inc=1, device_id={'sh': lax.rem(me + d, n)}, device_id_type=MESH)

    ins, outs = (k_in, v_in), (k_out, v_out)

    def over_load(a, e):
        return pltpu.make_async_copy(ins[a].at[:, pl.ds(e * WINDOW, over)], (over_a, over_b)[e].at[a], over_sem.at[a, e])

    def own_load(a):
        return pltpu.make_async_copy(ins[a].at[:, pl.ds(first * group, nst * group)], staged.at[a], stage_sem.at[a, 0])

    def other_load(a):
        return pltpu.make_async_copy(ins[a].at[:, pl.ds(half * group, nst * group)], kv_buf.at[:, pl.ds(a * nst * group, nst * group)], stage_sem.at[a, 1])
    for a in (0, 1):
        if nst:
            own_load(a).start()
            other_load(a).start()
        for e in (0, 1):
            over_load(a, e).start()
    depth, wide = wbuf.shape[1], wbuf.shape[2]
    wsteps = wq.shape[0] // depth
    weights = ((wq, 0), (wk, wq.shape[1]), (wv, wq.shape[1] + wk.shape[1]))

    def w_load(step, slot, i):
        src, at = weights[i]
        return pltpu.make_async_copy(src.at[pl.ds(pl.multiple_of(step * depth, depth), depth), :], wbuf.at[slot, :, pl.ds(at, src.shape[1])], w_sem.at[slot, i])
    for i in range(3):
        w_load(0, 0, i).start()
    pl.semaphore_wait(barrier, n - 1)

    tail = min(2 * group, max(first * group - over, 0))
    cut = first * group - tail
    parts = {}
    for a in (0, 1):
        parts[a, 'first'] = (over_a.at[a], 0, 0, over)
        if nst:
            parts[a, 'mixed'] = (staged.at[a], 0, first * group, nst * group)
        if cut > over:
            parts[a, 'plain'] = (ins[a], over, over, cut - over)
        if tail:
            parts[a, 'tail'] = (ins[a], cut, cut, tail)
    index = {key: i for i, key in enumerate(parts)}
    order = (2, 6, 3, 5, 4, 7, 1)

    def send(key, d):
        src, at, to, size = parts[key]
        peer = lax.rem(me + d, n)
        return pltpu.make_async_remote_copy(
            src_ref=src.at[peer, pl.ds(at, size)], dst_ref=outs[key[0]].at[me, pl.ds(to, size)],
            send_sem=send_sem.at[d, index[key]], recv_sem=recv_sem.at[d, index[key]], device_id={'sh': peer}, device_id_type=MESH)

    def own(key):
        src, at, to, size = parts[key]
        return pltpu.make_async_copy(src.at[me, pl.ds(at, size)], outs[key[0]].at[me, pl.ds(to, size)], own_sem.at[index[key]])

    def launch(key):
        if key in parts:
            for d in order:
                send(key, d).start()
            own(key).start()

    def arrived(key):
        if key in parts:
            own(key).wait()
            for d in order:
                send(key, d).wait_recv()

    launch((0, 'plain'))
    launch((0, 'tail'))
    for a in (0, 1):
        for e in (0, 1):
            over_load(a, e).wait()

        def put_first(r, c):
            slot = lax.broadcasted_iota(jnp.int32, over_a.shape[2:], 0)
            over_a[a, r] = jnp.where(slot < len_ref[r] - WINDOW, over_b[a, r], over_a[a, r])
            return c
        lax.fori_loop(0, n, put_first, 0)
        if nst:
            own_load(a).wait()
            other_load(a).wait()

            def put_mixed(i, c):
                r, j = lax.div(i, nst), lax.rem(i, nst)
                blocks = lax.div(jnp.minimum(len_ref[r], WINDOW) + group - 1, group)
                other = kv_buf[r + 1 - 2 * lax.rem(r, 2), pl.ds(pl.multiple_of((a * nst + nst - 1 - j) * group, group), group), :]
                at = pl.ds(pl.multiple_of(j * group, group), group)
                staged[a, r, at, :] = jnp.where(first + j < blocks, staged[a, r, at, :], other)
                return c
            lax.fori_loop(0, n * nst, put_mixed, 0)
    launch((0, 'mixed'))
    launch((0, 'first'))
    launch((1, 'mixed'))
    launch((1, 'first'))
    launch((1, 'plain'))
    launch((1, 'tail'))

    x = x_ref[...].astype(jnp.float32)
    inv_rms = lax.rsqrt(jnp.mean(x * x, axis=-1, keepdims=True) + EPS)
    normed[...] = (x * inv_rms * g_ref[...].astype(jnp.float32)).astype(normed.dtype)
    proj[...] = jnp.zeros_like(proj)
    strip = 1024

    def project(step, c):
        slot = lax.rem(step, 2)

        @pl.when(step + 1 < wsteps)
        def _():
            for i in range(3):
                w_load(step + 1, 1 - slot, i).start()
        for i in range(3):
            w_load(step, slot, i).wait()
        h = normed[:, pl.ds(pl.multiple_of(step * depth, depth), depth)]

        def one(s, c):
            at = pl.ds(pl.multiple_of(s * strip, strip), strip)
            proj[:, at] += jnp.dot(h, wbuf[slot, :, at], preferred_element_type=jnp.float32)
            return c
        return lax.fori_loop(0, wide // strip, one, c)
    lax.fori_loop(0, wsteps, project, 0)
    for j in range(wide // head_dim):
        proj2[pl.ds(j, 1), :] = proj[:, pl.ds(j * head_dim, head_dim)]
    cos_row, sin_row = cos_ref[pl.ds(me, 1), :], sin_ref[pl.ds(me, 1), :]

    def turn(value):
        value = value.astype(jnp.bfloat16).astype(jnp.float32)
        return (value * cos_row + pltpu.roll(value, head_dim // 2, 1) * sin_row).astype(jnp.bfloat16)
    nq = heads * q_group
    turned = turn(proj2[pl.ds(0, nq), :])
    for h in range(heads):
        q_heads[h] = turned[h * q_group:(h + 1) * q_group]
    k_turned = turn(proj2[pl.ds(nq, heads), :])
    k_new[...] = k_turned
    for h in range(heads):
        k_rows32[h] = k_turned[h:h + 1].astype(jnp.float32)
    v_new[...] = proj2[pl.ds(nq + heads, heads), :].astype(jnp.bfloat16)

    def forward(a, head, j):
        return pltpu.make_async_remote_copy(
            src_ref=outs[a].at[head, pl.ds(pl.multiple_of(j * group, group), group)],
            dst_ref=outs[a].at[head, pl.ds(pl.multiple_of((2 * half - 1 - j) * group, group), group)],
            send_sem=fsend_sem.at[a], recv_sem=frecv_sem.at[a], device_id={'sh': mate}, device_id_type=MESH)

    def pass_on(a):
        for d in (0, 7, 1, 2, 6, 3, 5, 4):
            if d == 0:
                own((a, 'mixed')).wait()
            else:
                send((a, 'mixed'), d).wait_recv()
            head = lax.rem(me - d + n, n)

            def go(j, c):
                forward(a, head, j).start()
                return c
            lax.fori_loop(first, half, go, 0)

    def passed(a):
        return pltpu.make_async_remote_copy(
            src_ref=outs[a].at[:, pl.ds(first * group, nst * group)], dst_ref=outs[a].at[:, pl.ds(half * group, nst * group)],
            send_sem=fsend_sem.at[a], recv_sem=frecv_sem.at[a], device_id={'sh': mate}, device_id_type=MESH)

    def load(a, lo, hi):
        copy = pltpu.make_async_copy(outs[a].at[:, pl.ds(lo, hi - lo)], kv_buf.at[:, pl.ds(lo, hi - lo)], kv_sem)
        copy.start()
        copy.wait()

    piece = group

    def each(lo, hi, step):
        count = (hi - lo) // piece

        def one(i, c):
            step(lax.div(i, count), pl.ds(pl.multiple_of(lo + lax.rem(i, count) * piece, piece), piece))
            return c
        lax.fori_loop(0, heads * count, one, 0)

    def score(lo, hi):
        load(0, lo, hi)

        def step(h, at):
            scores[h, :, at] = lax.dot_general(q_heads[h], kv_buf[h, at, :], (((1,), (1,)), ((), ())), preferred_element_type=jnp.float32)
        each(lo, hi, step)

    def gather(lo, hi):
        load(1, lo, hi)

        def step(h, at):
            acc[h] += jnp.dot(probs[h, :, at], kv_buf[h, at, :], preferred_element_type=jnp.float32)
        each(lo, hi, step)

    arrived((0, 'plain'))
    arrived((0, 'tail'))
    if first * group > over:
        score(over, first * group)
    if nst:
        pass_on(0)
        score(first * group, half * group)
    arrived((0, 'first'))
    score(0, over)
    if nst:
        passed(0).wait_recv()
        score(half * group, WINDOW)

    length = len_ref[me]
    fresh = lax.rem(length, WINDOW)

    def soften(h, c):
        slot = lax.broadcasted_iota(jnp.int32, (q_group, WINDOW), 1)
        s_new = jnp.sum(q_heads[h].astype(jnp.float32) * k_rows32[h], axis=-1, keepdims=True)
        s = jnp.where(slot == fresh, s_new, scores[h]) / head_dim ** 0.5
        s = jnp.where(slot <= length, s, -jnp.inf)
        e = jnp.exp(s - jnp.max(s, axis=-1, keepdims=True))
        p = e / jnp.sum(e, axis=-1, keepdims=True)
        p_new[h] = jnp.broadcast_to(jnp.sum(jnp.where(slot == fresh, p, 0.0), axis=-1, keepdims=True), (q_group, head_dim))
        probs[h] = jnp.where(slot == fresh, 0.0, p).astype(probs.dtype)
        acc[h] = jnp.zeros_like(acc[h])
        return c
    lax.fori_loop(0, heads, soften, 0)

    if nst:
        pass_on(1)
        gather(first * group, half * group)
        passed(1).wait_recv()
        gather(half * group, WINDOW)
    arrived((1, 'first'))
    gather(0, over)
    arrived((1, 'plain'))
    if cut > over:
        gather(over, cut)
    arrived((1, 'tail'))
    if tail:
        gather(cut, cut + tail)
    for h in range(heads):
        o = acc[h] + p_new[h].astype(jnp.bfloat16).astype(jnp.float32) * v_new[pl.ds(h, 1), :].astype(jnp.float32)
        for g in range(q_group):
            flat[:, pl.ds((h * q_group + g) * head_dim, head_dim)] = o[g:g + 1].astype(flat.dtype)
    for key in parts:
        for d in order:
            send(key, d).wait_send()
    if nst:
        for a in (0, 1):
            passed(a).wait_send()


def exchange(n, group, half, lengths, residual, norm_gain, cos_rows, sin_rows, k_rows, v_rows, w_query, w_key, w_value):
    rows, seq, head_dim = k_rows.shape
    over = seq - WINDOW
    kv_heads = w_key.shape[1] // head_dim
    q_group = w_query.shape[1] // w_key.shape[1]
    wide = w_query.shape[1] + w_key.shape[1] + w_value.shape[1]
    depth = 256
    nst = WINDOW // group - half
    bf16, f32 = k_rows.dtype, jnp.float32
    out = jax.ShapeDtypeStruct((n, WINDOW, head_dim), bf16)
    new = jax.ShapeDtypeStruct((kv_heads, head_dim), bf16)
    any_spec = pl.BlockSpec(memory_space=pl.ANY)
    vmem = pl.BlockSpec(memory_space=pltpu.VMEM)
    dma = pltpu.SemaphoreType.DMA
    return pl.pallas_call(
        functools.partial(exchange_kernel, n, group, half),
        out_shape=(out, out, jax.ShapeDtypeStruct((1, w_query.shape[1]), bf16), new, new),
        in_specs=[pl.BlockSpec(memory_space=pltpu.SMEM)] + [vmem] * 4 + [any_spec] * 5,
        out_specs=(any_spec, any_spec, vmem, vmem, vmem),
        scratch_shapes=[
            pltpu.VMEM((2, rows, over, head_dim), bf16), pltpu.VMEM((2, rows, over, head_dim), bf16),
            pltpu.VMEM((2, rows, max(nst, 1) * group, head_dim), bf16),
            pltpu.VMEM((n, WINDOW, head_dim), bf16),
            pltpu.VMEM((2, depth, wide), bf16),
            pltpu.VMEM((1, w_query.shape[0]), bf16), pltpu.VMEM((1, wide), f32), pltpu.VMEM((wide // head_dim, head_dim), f32),
            pltpu.VMEM((kv_heads, q_group, head_dim), bf16),
            pltpu.VMEM((kv_heads, q_group, WINDOW), f32), pltpu.VMEM((kv_heads, q_group, WINDOW), bf16),
            pltpu.VMEM((kv_heads, q_group, head_dim), f32), pltpu.VMEM((kv_heads, q_group, head_dim), f32), pltpu.VMEM((kv_heads, 1, head_dim), f32),
            dma((n, 8)), dma((n, 8)), dma((8,)), dma((2,)), dma((2,)), dma((2, 2)), dma((2, 2)), dma((2, 3)), dma,
        ],
        compiler_params=pltpu.CompilerParams(collective_id=0, has_side_effects=True, vmem_limit_bytes=VMEM_EXCHANGE),
        name=f'exchange{half}',
    )(lengths, residual, norm_gain, cos_rows, sin_rows, k_rows, v_rows, w_query, w_key, w_value)


def finish_kernel(blk, len_ref, k_in, v_in, kn_ref, vn_ref, perm_ref, x_ref, flat_ref, w_ref, k_out, v_out, x_out, total):
    step = pl.program_id(0)
    heads, _, head_dim = k_in.shape
    length = len_ref[0]
    fresh = lax.rem(length, WINDOW)
    part = perm_ref.shape[0] // heads
    base = step * blk
    wblk = w_ref.shape[0]

    @pl.when(step == 0)
    def _():
        total[...] = x_ref[...].astype(jnp.float32)
    at = pl.multiple_of(step * wblk, wblk)
    total[...] += jnp.dot(flat_ref[:, pl.ds(at, wblk)], w_ref[...], preferred_element_type=jnp.float32)

    for src, new, dst in ((k_in, kn_ref, k_out), (v_in, vn_ref, v_out)):
        new_rows = jnp.tile(new[...].astype(jnp.float32), (part, 1))
        for g in range(0, blk // part, 2):
            pair = jnp.concatenate([src[:, pl.ds((g + e) * part, part), :].reshape(heads * part, head_dim) for e in (0, 1)], axis=1)
            mixed = jnp.dot(perm_ref[...], pair, preferred_element_type=jnp.float32)
            for e in (0, 1):
                row = lax.broadcasted_iota(jnp.int32, (heads * part, head_dim), 0) + (base + (g + e) * part) * heads
                value = mixed[:, e * head_dim:(e + 1) * head_dim]
                value = jnp.where(row < length * heads, value, 0.0)
                value = jnp.where((row >= fresh * heads) & (row < (fresh + 1) * heads), new_rows, value)
                dst[pl.ds((g + e) * part * heads, part * heads), :] = value.astype(dst.dtype)

    @pl.when(step == pl.num_programs(0) - 1)
    def _():
        x_out[...] = total[...].astype(x_out.dtype)


def finish(my_len, k_heads, v_heads, k_new, v_new, residual, flat, w_out):
    heads, _, head_dim = k_heads.shape
    width, dim = w_out.shape
    blk, part = 256, 256 // heads
    steps = WINDOW // blk
    row = jnp.arange(part * heads)
    perm = (row[None, :] == (row % heads * part + row // heads)[:, None]).astype(k_heads.dtype)
    cache = jax.ShapeDtypeStruct((WINDOW * heads, head_dim), k_heads.dtype)
    whole = lambda a: pl.BlockSpec(a.shape, lambda i, *_: (0,) * a.ndim)
    return pl.pallas_call(
        functools.partial(finish_kernel, blk),
        grid_spec=pltpu.PrefetchScalarGridSpec(
            num_scalar_prefetch=1, grid=(steps,),
            in_specs=[
                pl.BlockSpec((heads, blk, head_dim), lambda i, *_: (0, i, 0)),
                pl.BlockSpec((heads, blk, head_dim), lambda i, *_: (0, i, 0)),
                whole(k_new), whole(v_new), whole(perm), whole(residual), whole(flat),
                pl.BlockSpec((width // steps, dim), lambda i, *_: (i, 0)),
            ],
            out_specs=[
                pl.BlockSpec((blk * heads, head_dim), lambda i, *_: (i, 0)),
                pl.BlockSpec((blk * heads, head_dim), lambda i, *_: (i, 0)),
                pl.BlockSpec((1, dim), lambda i, *_: (0, 0)),
            ],
            scratch_shapes=[pltpu.VMEM((1, dim), jnp.float32)]),
        out_shape=(cache, cache, jax.ShapeDtypeStruct(residual.shape, residual.dtype)),
        compiler_params=pltpu.CompilerParams(dimension_semantics=('arbitrary',), vmem_limit_bytes=VMEM_FINISH),
        cost_estimate=pl.CostEstimate(flops=10 ** 9, bytes_accessed=64 << 20, transcendentals=0),
        name='finish',
    )(my_len, k_heads, v_heads, k_new, v_new, perm, residual, flat, w_out)


GROUP = 256
VMEM_EXCHANGE = 28 << 20
VMEM_FINISH = 20 << 20


def solution(mesh):
    head_spec = P('dp', None, 'sh', None)
    row_spec = P(('dp', 'sh'))
    full_spec = P(None, None)
    n = mesh.shape['sh']

    def per_device(k_prefill, v_prefill, lengths, residual, norm_gain, w_query, w_key, w_value, w_out):
        num_rows = residual.shape[0]
        rows, seq, _, head_dim = k_prefill.shape
        kv_heads = w_key.shape[1] // head_dim
        half_dim = head_dim // 2
        my_len = lax.dynamic_slice_in_dim(lengths, lax.axis_index('sh') * num_rows, num_rows)
        k_rows = k_prefill.reshape(rows, seq, head_dim)
        v_rows = v_prefill.reshape(rows, seq, head_dim)
        blocks = (jnp.minimum(lengths, WINDOW) + GROUP - 1) // GROUP
        need = (jnp.max(blocks.reshape(-1, 2).sum(axis=1)) + 1) // 2
        level = jnp.maximum(need - levels(GROUP)[0], 0)
        inv_freq = THETA ** (-2.0 * jnp.arange(half_dim, dtype=jnp.float32) / head_dim)
        angles = lengths.astype(jnp.float32)[:, None] * inv_freq
        cos_rows = jnp.concatenate([jnp.cos(angles), jnp.cos(angles)], axis=1)
        sin_rows = jnp.concatenate([-jnp.sin(angles), jnp.sin(angles)], axis=1)
        k_heads, v_heads, flat, k_new, v_new = lax.switch(
            level, [functools.partial(exchange, n, GROUP, half) for half in levels(GROUP)],
            lengths, residual, norm_gain[None], cos_rows, sin_rows, k_rows, v_rows, w_query, w_key, w_value)
        k_cache, v_cache, resid_out = finish(my_len, k_heads, v_heads, k_new, v_new, residual, flat, w_out)
        cache_shape = (num_rows, WINDOW, kv_heads, head_dim)
        return resid_out, k_cache.reshape(cache_shape), v_cache.reshape(cache_shape)
    return jax.shard_map(per_device, mesh=mesh, in_specs=(head_spec, head_spec, P('dp'), P(('dp', 'sh'), None), P(None), full_spec, full_spec, full_spec, full_spec), out_specs=(P(('dp', 'sh'), None), row_spec, row_spec), check_vma=False)
```

time: 377 us -> 198 us (0.53)
  the two profiles are of different devices: /device:TPU:112 before, /device:TPU:120 now
where the time goes in v2:
time: 198 us; the launch traced here: 197 us
  Pallas kernels  180 us (91%)
  local copies, waits for them, and re-layouts  12.6 us (6%)
    pallas_call x1, Pallas kernels, exchange(): pl.pallas_call(functools.partial(exchange_kernel, n, group, half), out_sh...  158 us
    pallas_call x1, Pallas kernels, finish(): pl.pallas_call(functools.partial(finish_kernel, blk), grid_spec=pltpu.Pre...  22.8 us
    unnamed x2, local copies, waits for them, and re-layouts  10.5 us

profile of v2, /device:TPU:120, one launch (start us, length us, event | category | flops | bytes accessed | tf_op | source)
XLA Modules:
  0.0 196.9 jit_solution(11901663838685529859)
XLA Ops:
  0.6 0.7 fusion.6
  1.4 0.1 reshape.49
  1.5 0.1 reduce_sum.9
  1.6 0.6 reduce_max.9
  2.9 0.1 fusion.5
  3.0 0.1 pad_maximum_fusion
  3.1 0.7 broadcast_in_dim.2
  3.8 158.2 %conditional.1 = ((bf16[8,4096,128]{2,1,0:T(8,128)(2,1)}, bf16[8,4096,128]{2,1,0:T(8,128)(2,1)}, bf16[1,4096]{1,0:T(2,128)(2,1)S(1)}, bf16[8,128]{1,0:T(8,128)(2,1)S(1)}, bf16[8,128]{1,0:T(8,128)(2,1)S(1)})) conditional(s32[]{:T(128)} %clamp.3, (s32[8]{0:T(128)}, bf16[1,4096]{1,0:T(2,128)(2,1)}, ...), branch_computations={%region_2.3_spmd, %region_3.4_spmd, %region_4.5_spmd, %region_5.6_... | conditional | bytes 8 | solution.py:402
  4.0 157.5 %exchange13.1 = (bf16[8,4096,128]{2,1,0:T(8,128)(2,1)}, bf16[8,4096,128]{2,1,0:T(8,128)(2,1)}, bf16[1,4096]{1,0:T(2,128)(2,1)S(1)}, bf16[8,128]{1,0:T(8,128)(2,1)S(1)}, bf16[8,128]{1,0:T(8,128)(2,1)S(1)}) custom-call(s32[8]{0:T(128)} %get-tuple-element.200.len_ref, bf16[1,4096]{1,0:T(2,128)(2,1)} %get-tuple-element.201.x_ref, ...), custom_call_target="tpu_custom_call" | custom-call | tf_op jit(solution)/shard_map/cond/branch_4_fun/exchange13/pallas_call | solution.py:291
  162.1 1.3 dynamic_slice.3.len_ref
  163.3 0.1 fusion.perm_ref
  163.4 0.0 copy-start
  163.4 10.5 %copy-done = bf16[4096,4096]{1,0:T(8,128)(2,1)S(1)} copy-done((bf16[4096,4096]{1,0:T(8,128)(2,1)S(1)}, bf16[4096,4096]{1,0:T(8,128)(2,1)}, u32[]{:S(2)}) %copy-start) | copy-done | bytes 33554456
  174.0 22.8 %finish.1 = (bf16[32768,128]{1,0:T(8,128)(2,1)}, bf16[32768,128]{1,0:T(8,128)(2,1)}, bf16[1,4096]{1,0:T(2,128)(2,1)}) custom-call(s32[1]{0:T(128)} %dynamic_slice.3.len_ref, bf16[8,4096,128]{2,1,0:T(8,128)(2,1)} %get-tuple-element.251.k_in, bf16[8,4096,128]{2,1,0:T(8,128)(2,1)} %get-tuple-element.252.v_in, bf16[8,128]{1,0:T(8,128)(2,1)S(1)} %get-tuple-element.253.kn_ref, ...), custom_call_target="tpu_custom_call" | custom-call | flops 1000000000 | bytes 67108864 | tf_op jit(solution)/shard_map/finish/pallas_call | solution.py:353
  (2 shorter events, 0.0 us)
Async XLA Ops:
  163.4 10.5 %copy-start = (bf16[4096,4096]{1,0:T(8,128)(2,1)S(1)}, bf16[4096,4096]{1,0:T(8,128)(2,1)}, u32[]{:S(2)}) copy-start(bf16[4096,4096]{1,0:T(8,128)(2,1)} %w_ref.1) | copy-start | bytes 100663296
